TPU v7x, 32 devices: a whole 2x2x4 slice. The times are simulated.
32 devices in a mesh: section: 2 (over y), dp: 16 (over z, x, core).
Axes of the slice: x: 2, y: 2, z: 4, core: 2. Of those that a mesh axis runs over, the one named last changes fastest.
Arguments:
- activations: bfloat16 [2, 4, 16, 14336], P('section', None, 'dp'), may hold values from -6 to 6
- out_grads: bfloat16 [2, 4, 16, 4096], P('section', None, 'dp'), may hold values from -6 to 6
- basis_in: bfloat16 [2, 14336, 1024], P('section', 'dp'), may hold values from -0.046875 to 0.046875
- basis_out: bfloat16 [2, 4096, 1024], P('section', 'dp'), may hold values from -0.09375 to 0.09375
- eigen_values: float32 [2, 1024, 1024], P('section', 'dp'), may hold values from 0.02 to 2
- query_proj: bfloat16 [2, 8, 1024, 1024], P('section', None, 'dp'), may hold values from -0.046875 to 0.046875
- lengths: int32 [4], replicated, may hold values from 4 to 16
- seq_rows: int32 [4], replicated, may hold values from 0 to 127
- prior_table: float32 [128, 8], P('dp'), may hold values from -6 to 6
Outputs:
- influence: float32 [2, 128, 8], P('section', 'dp')
All inputs are finite; a program needn't handle non-finite values.
Results may differ from a plain program's by a relative error of at most 0.01.
Values may be sent and summed in bfloat16 or wider, within the bound.
No kernel may reach another device: no remote copies, remote signals or barrier semaphores. Data moves between devices by JAX's collectives and lax.ppermute only.
A program may use at most 64 MiB of HBM per device.

v0:
```python
import jax
import jax.numpy as jnp
from jax import lax
from jax.sharding import PartitionSpec as P

DAMPING = 0.01


def entering(value, axis, join, neutral):
    count, mine = (lax.axis_size(axis), lax.axis_index(axis))
    pieces = lax.all_gather(value, axis)
    running = jnp.full_like(value, 0) + jnp.asarray(neutral, value.dtype)

    def step(position, running):
        longer = join(running, pieces[position])
        return jnp.where(position < mine, longer, running)

    return lax.fori_loop(0, count - 1, step, running)


def add_pair(earlier, latter):
    return earlier + latter


def per_device(
    activations,
    out_grads,
    basis_in,
    basis_out,
    eigen_values,
    query_proj,
    lengths,
    seq_rows,
    prior_table,
):
    micro = activations.shape[1]
    cols_acts, cols_grads = (
        lax.all_to_all(activations[0], "dp", split_axis=2, concat_axis=1, tiled=True),
        lax.all_to_all(out_grads[0], "dp", split_axis=2, concat_axis=1, tiled=True),
    )
    slots = cols_acts.shape[1]
    rank_size = basis_in.shape[2]
    act_part = jnp.dot(
        cols_acts.reshape(micro * slots, cols_acts.shape[2]),
        basis_in[0],
        preferred_element_type=jnp.float32,
    )
    grad_part = jnp.dot(
        cols_grads.reshape(micro * slots, cols_grads.shape[2]),
        basis_out[0],
        preferred_element_type=jnp.float32,
    )
    grad_share = lax.psum_scatter(grad_part, "dp", scatter_dimension=1, tiled=True).astype(
        jnp.bfloat16
    )
    act_proj = lax.psum(act_part, "dp").astype(jnp.bfloat16)
    block_rows = grad_share.shape[1]
    position = jnp.arange(slots, dtype=jnp.int32)
    live_mask = (position[None, :] < lengths[:, None]).reshape(micro * slots, 1)
    grad_share = jnp.where(live_mask, grad_share, jnp.zeros_like(grad_share))
    inverse_len = 1.0 / lengths.astype(jnp.float32)
    seq_block = (
        jnp.einsum(
            "mti,mtj->mij",
            grad_share.reshape(micro, slots, block_rows),
            act_proj.reshape(micro, slots, rank_size),
            preferred_element_type=jnp.float32,
        )
        * inverse_len[:, None, None]
    )
    precond = (query_proj[0].astype(jnp.float32) / (eigen_values[0][None] + DAMPING)).astype(
        jnp.bfloat16
    )
    partial_value = jnp.einsum(
        "mij,qij->mq", seq_block, precond.astype(jnp.float32), precision=lax.Precision.HIGHEST
    )
    table_rows = prior_table.shape[0]
    first_row = lax.axis_index("dp") * table_rows
    summed = lax.psum(partial_value, "dp")
    before = entering(summed, "section", add_pair, jnp.zeros_like(summed))
    owner_mask = (
        seq_rows[None, :] == (first_row + jnp.arange(table_rows, dtype=jnp.int32))[:, None]
    ).astype(jnp.float32)
    result = prior_table + jnp.dot(owner_mask, before + summed, precision=lax.Precision.HIGHEST)
    return result[None]


def solution(mesh):
    return jax.shard_map(
        per_device,
        mesh=mesh,
        in_specs=(
            P("section", None, "dp", None),
            P("section", None, "dp", None),
            P("section", "dp", None),
            P("section", "dp", None),
            P("section", "dp", None),
            P("section", None, "dp", None),
            P(),
            P(),
            P("dp", None),
        ),
        out_specs=P("section", "dp", None),
        check_vma=False,
    )
```

profile of v0, /device:TPU:0, one launch (start us, length us, event | category | flops | bytes accessed | tf_op | source)
XLA Modules:
  0.0 303.3 jit_solution(3628222360008374152)
XLA Ops:
  6.5 0.0 copy-start
  6.5 5.0 %copy.14 = bf16[4,1,4096]{0,1,2:T(2,128)(2,1)} copy(bf16[4,1,4096]{2,0,1:T(4,128)(2,1)} %bitcast.47) | data formatting | bytes 65536 | tf_op jit(solution)/shard_map/squeeze | solution.py:39
  11.5 0.5 broadcast.36
  12.1 23.5 %reduce = bf16[4096,4]{1,0:T(8,128)(2,1)S(1)} reduce(bf16[4096,1,4]{2,1,0:T(2,128)(2,1)} %bitcast.42, bf16[]{:T(256)} %broadcast.36), dimensions={1}, to_apply=%bitcast.32.reduce_sub_computation | reduce | bytes 65538
  35.5 2.6 reshape.67
  38.1 7.4 %all-to-all-start = ((bf16[16,2,512]{2,1,0:T(2,128)(2,1)}), bf16[16,2,512]{2,1,0:T(2,128)(2,1)S(1)}, u32[]{:S(2)}, u32[]{:S(2)}) async-start(bf16[16,2,512]{2,1,0:T(2,128)(2,1)} %reshape.67), calls=%async_computation | async-start | bytes 65536 | tf_op jit(solution)/shard_map/all_to_all | solution.py:39
  45.5 0.0 copy-done.7
  45.6 0.1 iota_compare_fusion
  45.6 0.5 convert_divide_fusion.1
  46.2 0.0 copy-done.3
  46.2 11.6 %copy.16 = bf16[4,1,14336]{0,1,2:T(2,128)(2,1)} copy(bf16[4,1,14336]{2,0,1:T(4,128)(2,1)S(1)} %bitcast.45) | data formatting | bytes 229376 | tf_op jit(solution)/shard_map/squeeze | solution.py:38
  57.7 79.8 %reduce.1 = bf16[14336,4]{1,0:T(8,128)(2,1)} reduce(bf16[14336,1,4]{2,1,0:T(2,128)(2,1)} %bitcast.41, bf16[]{:T(256)} %broadcast.36), dimensions={1}, to_apply=%bitcast.34.reduce_sub_computation | reduce | bytes 229378
  137.6 8.3 %reshape.69 = bf16[16,2,1792]{2,1,0:T(2,128)(2,1)} reshape(bf16[14336,4]{1,0:T(8,128)(2,1)} %reduce.1) | data formatting | bytes 229376
  145.8 0.6 lt.31
  146.4 0.0 copy-done.2
  146.5 1.5 fusion
  148.0 0.5 iota_add_fusion
  148.6 0.0 all-to-all-done
  148.6 6.0 %all-to-all-start.1 = ((bf16[16,2,1792]{2,1,0:T(2,128)(2,1)}), bf16[16,2,1792]{2,1,0:T(2,128)(2,1)S(1)}, u32[]{:S(2)}, u32[]{:S(2)}) async-start(bf16[16,2,1792]{2,1,0:T(2,128)(2,1)} %reshape.69), calls=%async_computation.1 | async-start | bytes 229376 | tf_op jit(solution)/shard_map/all_to_all | solution.py:38
  154.6 0.0 copy-start.1
  154.6 0.0 reduce-scatter.4.cloned.1.call-start
  154.6 4.5 %reshape.68 = bf16[4096,1,4]{2,1,0:T(2,128)(2,1)} reshape(bf16[16,2,512]{2,1,0:T(2,128)(2,1)S(1)} %all-to-all-done) | data formatting | bytes 65536
  159.2 4.5 %copy.15 = bf16[4,1,4096]{2,0,1:T(4,128)(2,1)S(1)} copy(bf16[4,1,4096]{0,1,2:T(2,128)(2,1)} %bitcast.43) | data formatting | bytes 65536 | tf_op jit(solution)/shard_map/all_to_all | solution.py:39
  163.7 0.6 reshape.47
  164.3 0.0 copy-done.1
  164.4 1.9 convolution_bitcast_fusion
  166.2 0.0 reduce-scatter.4.cloned.1.call-update
  166.3 0.0 all-to-all-done.1
  166.3 11.5 %reshape.70 = bf16[14336,1,4]{2,1,0:T(2,128)(2,1)} reshape(bf16[16,2,1792]{2,1,0:T(2,128)(2,1)S(1)} %all-to-all-done.1) | data formatting | bytes 229376
  177.8 13.9 %copy.17 = bf16[4,1,14336]{2,0,1:T(4,128)(2,1)S(1)} copy(bf16[4,1,14336]{0,1,2:T(2,128)(2,1)} %bitcast.40) | data formatting | bytes 229376 | tf_op jit(solution)/shard_map/all_to_all | solution.py:38
  191.7 0.0 copy-start.5
  191.8 0.1 reshape.49
  191.9 0.4 fusion.1
  192.3 0.0 copy-start.6
  192.3 0.0 copy-start.8
  192.3 0.0 copy-start.9
  192.3 64.6 %all-reduce.1 = bf16[64,1024]{1,0:T(8,128)(2,1)S(1)} all-reduce(f32[64,1024]{1,0:T(8,128)S(1)} %fusion.1), channel_id=1, replica_groups=mesh['section'=2,'dp'=16] {'dp'}, use_global_device_ids=true, to_apply=%region_1.0 | all-reduce | flops 65536 | bytes 393216 | tf_op jit(solution)/shard_map/psum | solution.py:56
  256.9 0.0 reduce-scatter.4.cloned.1.call-done
  257.0 0.8 copy.21
  257.8 0.0 copy-done.5
  257.8 0.1 convert_select_fusion
  257.9 0.0 copy-done.4
  257.9 0.3 convolution_multiply_fusion
  258.3 3.5 %convolution_bitcast_fusion.1 = f32[4,8]{1,0:T(4,128)S(1)} fusion(bf16[8,64,1024]{2,1,0:T(8,128)(2,1)S(1)} %fusion, f32[4,64,1024]{2,1,0:T(8,128)S(1)} %convolution_multiply_fusion), kind=kOutput, calls=%fused_computation.8 | convolution fusion | flops 25165824 | bytes 2097280 | tf_op jit(solution)/shard_map/mij,qij->mq/dot_general | solution.py:74
  261.8 29.5 %psum.15 = f32[4,8]{1,0:T(4,128)S(1)} all-reduce(f32[4,8]{1,0:T(4,128)S(1)} %convolution_bitcast_fusion.1), channel_id=1, replica_groups=mesh['section'=2,'dp'=16] {'dp'}, use_global_device_ids=true, to_apply=%region_2.3 | all-reduce | flops 32 | bytes 256 | tf_op jit(solution)/shard_map/psum | solution.py:79
  291.3 4.4 %all-gather.1 = f32[2,4,8]{2,1,0:T(4,128)S(1)} all-gather(f32[1,4,8]{2,1,0:T(4,128)S(1)} %bitcast.49), channel_id=2, replica_groups=mesh['section'=2,'dp'=16] {'section'}, dimensions={0}, use_global_device_ids=true | all-gather | bytes 384 | tf_op jit(solution)/shard_map/all_gather | solution.py:11
  295.6 0.0 copy-done.8
  295.6 0.8 fusion.3
  (8 shorter events, 0.0 us)
Async XLA Ops:
  6.5 185.3 %copy-start = (bf16[1,896,1024]{2,1,0:T(8,128)(2,1)S(1)}, bf16[1,896,1024]{2,1,0:T(8,128)(2,1)}, u32[]{:S(2)}) copy-start(bf16[1,896,1024]{2,1,0:T(8,128)(2,1)} %param.11) | copy-start | bytes 5505028
  12.1 33.5 %copy-start.7 = (s32[4]{0:T(128)S(1)}, s32[4]{0:T(128)}, u32[]{:S(2)}) copy-start(s32[4]{0:T(128)} %param.15) | copy-start | bytes 52
  12.1 34.1 %copy-start.3 = (bf16[1,4,1,14336]{3,1,2,0:T(4,128)(2,1)S(1)}, bf16[1,4,1,14336]{3,1,2,0:T(4,128)(2,1)}, u32[]{:S(2)}) copy-start(bf16[1,4,1,14336]{3,1,2,0:T(4,128)(2,1)} %param.9) | copy-start | bytes 344068
  38.1 110.4 %all-to-all-start = ((bf16[16,2,512]{2,1,0:T(2,128)(2,1)}), bf16[16,2,512]{2,1,0:T(2,128)(2,1)S(1)}, u32[]{:S(2)}, u32[]{:S(2)}) async-start(bf16[16,2,512]{2,1,0:T(2,128)(2,1)} %reshape.67), calls=%async_computation | async-start | bytes 65536 | tf_op jit(solution)/shard_map/all_to_all | solution.py:39
  137.6 8.9 %copy-start.2 = (f32[1,64,1024]{2,1,0:T(8,128)S(1)}, f32[1,64,1024]{2,1,0:T(8,128)}, u32[]{:S(2)}) copy-start(f32[1,64,1024]{2,1,0:T(8,128)} %param.13) | copy-start | bytes 786436
  148.6 17.7 %all-to-all-start.1 = ((bf16[16,2,1792]{2,1,0:T(2,128)(2,1)}), bf16[16,2,1792]{2,1,0:T(2,128)(2,1)S(1)}, u32[]{:S(2)}, u32[]{:S(2)}) async-start(bf16[16,2,1792]{2,1,0:T(2,128)(2,1)} %reshape.69), calls=%async_computation.1 | async-start | bytes 229376 | tf_op jit(solution)/shard_map/all_to_all | solution.py:38
  154.6 9.8 %copy-start.1 = (bf16[1,256,1024]{2,1,0:T(8,128)(2,1)S(1)}, bf16[1,256,1024]{2,1,0:T(8,128)(2,1)}, u32[]{:S(2)}) copy-start(bf16[1,256,1024]{2,1,0:T(8,128)(2,1)} %param.12) | copy-start | bytes 1572868
  154.6 102.4 %reduce-scatter.4.cloned.1.call-start = ((), (), s32[]{:S(2)}) async-start(), calls=%async_computation.3 | async-start | bytes 557056
  191.7 66.1 %copy-start.5 = (pred[64]{0:T(512)(128)(4,1)S(1)}, pred[64]{0:T(512)(128)(4,1)}, u32[]{:S(2)}) copy-start(pred[64]{0:T(512)(128)(4,1)} %lt.31) | copy-start | bytes 196
  191.7 66.1 %copy-start.4 = (f32[4]{0:T(128)S(1)}, f32[4]{0:T(128)}, u32[]{:S(2)}) copy-start(f32[4]{0:T(128)} %convert_divide_fusion.1) | copy-start | bytes 52
  192.3 103.3 %copy-start.6 = (f32[8,8]{1,0:T(8,128)S(1)}, f32[8,8]{1,0:T(8,128)}, u32[]{:S(2)}) copy-start(f32[8,8]{1,0:T(8,128)} %param.17) | copy-start | bytes 772
  192.3 103.3 %copy-start.8 = (s32[4]{0:T(128)S(1)}, s32[4]{0:T(128)}, u32[]{:S(2)}) copy-start(s32[4]{0:T(128)} %param.16) | copy-start | bytes 52
  192.3 103.3 %copy-start.9 = (s32[8]{0:T(128)S(1)}, s32[8]{0:T(128)}, u32[]{:S(2)}) copy-start(s32[8]{0:T(128)} %iota_add_fusion) | copy-start | bytes 100
Sparse Core Ops, SparseCore 0:
  166.4 57.5 reduce-scatter.3
where the time goes:
time: 304 us; the launch traced here: 303 us
  other arithmetic  106 us (35%)
  blocking collectives  98.4 us (32%)
  local copies, waits for them, and re-layouts  64.7 us (21%)
  between operations  13.6 us (4%)
  starting transfers between devices  13.4 us (4%)
  matrix products  6.96 us (2%)
    unnamed x2, other arithmetic  103 us
    psum x1, blocking collectives, per_device(): act_proj = lax.psum(act_part, 'dp').astype(jnp.bfloat16)  64.6 us
    psum x1, blocking collectives, per_device(): summed = lax.psum(partial_value, 'dp')  29.5 us
    unnamed x26, local copies, waits for them, and re-layouts  28.3 us
    all_to_all x1, local copies, waits for them, and re-layouts, per_device(): lax.all_to_all(activations[0], 'dp', split_axis=2, concat_axis=1, tiled=T...  13.9 us
    squeeze x1, local copies, waits for them, and re-layouts, per_device(): activations[0]  11.6 us
    all_to_all x1, starting transfers between devices, per_device(): lax.all_to_all(out_grads[0], 'dp', split_axis=2, concat_axis=1, tiled=True)  7.39 us
  transfers between devices with their start and end apart: 3, of which 0 were waited for; matrix products, arithmetic and copies ran while one was open for 46% of the time, Pallas kernels for 0%

commit v1 on v0

--- a/solution.py
+++ b/solution.py
@@ -35,7 +35,12 @@
 ):
     micro = activations.shape[1]
     cols_acts, cols_grads = (
-        lax.all_to_all(activations[0], "dp", split_axis=2, concat_axis=1, tiled=True),
+        jnp.concatenate(
+            lax.all_to_all(
+                jnp.stack(jnp.split(activations[0], lax.axis_size("dp"), axis=2)), "dp", 0, 0
+            ),
+            axis=1,
+        ),
         lax.all_to_all(out_grads[0], "dp", split_axis=2, concat_axis=1, tiled=True),
     )
     slots = cols_acts.shape[1]

time: 304 us -> 188 us (0.62)
  other arithmetic: 106 us -> 26.2 us
  local copies, waits for them, and re-layouts: 64.7 us -> 28.8 us
    unnamed x2 -> x1, other arithmetic: 103 us -> 23.5 us
    all_to_all x1 -> x0, local copies, waits for them, and re-layouts: 13.9 us -> none  [per_device(): lax.all_to_all(activations[0], 'dp', split_axis=2, concat_axis=1, tiled=T...]
    squeeze x1 -> x0, local copies, waits for them, and re-layouts: 11.6 us -> none  [per_device(): activations[0]]
    unnamed x26 -> x39, local copies, waits for them, and re-layouts: 28.3 us -> 17.5 us
  transfers between devices with their start and end apart: 3 -> 3, of which waited for: 0 -> 0; matrix products, arithmetic and copies ran while one was open for 46% -> 13% of each run, Pallas kernels for 0% -> 0%
where the time goes in v1:
time: 188 us
  blocking collectives  98.5 us (52%)
  local copies, waits for them, and re-layouts  28.8 us (15%)
  other arithmetic  26.2 us (14%)
  between operations  13.6 us (7%)
  starting transfers between devices  13.4 us (7%)
  matrix products  6.99 us (4%)
    psum x1, blocking collectives, per_device(): act_proj = lax.psum(act_part, 'dp').astype(jnp.bfloat16)  64.7 us
    psum x1, blocking collectives, per_device(): summed = lax.psum(partial_value, 'dp')  29.5 us
    unnamed x1, other arithmetic  23.5 us
    unnamed x39, local copies, waits for them, and re-layouts  17.5 us
    all_to_all x1, starting transfers between devices, per_device(): lax.all_to_all(out_grads[0], 'dp', split_axis=2, concat_axis=1, tiled=True)  7.39 us
    all_to_all x1, starting transfers between devices, per_device(): lax.all_to_all(jnp.stack(jnp.split(activations[0], lax.axis_size('dp'), a...  6.01 us
    squeeze x1, local copies, waits for them, and re-layouts, per_device(): out_grads[0]  5 us
    all_to_all x1, local copies, waits for them, and re-layouts, per_device(): lax.all_to_all(out_grads[0], 'dp', split_axis=2, concat_axis=1, tiled=True)  4.53 us
  transfers between devices with their start and end apart: 3, of which 0 were waited for; matrix products, arithmetic and copies ran while one was open for 13% of the time, Pallas kernels for 0%

profile of v1, /device:TPU:0, one launch (start us, length us, event | category | flops | bytes accessed | tf_op | source)
XLA Modules:
  0.0 187.7 jit_solution(15974958571506428424)
XLA Ops:
  6.5 5.0 %copy.34 = bf16[4,1,4096]{0,1,2:T(2,128)(2,1)} copy(bf16[4,1,4096]{2,0,1:T(4,128)(2,1)} %bitcast.124) | data formatting | bytes 65536 | tf_op jit(solution)/shard_map/squeeze | solution.py:44
  11.5 0.5 broadcast.36
  12.1 23.5 %reduce = bf16[4096,4]{1,0:T(8,128)(2,1)S(1)} reduce(bf16[4096,1,4]{2,1,0:T(2,128)(2,1)} %bitcast.102, bf16[]{:T(256)} %broadcast.36), dimensions={1}, to_apply=%bitcast.96.reduce_sub_computation | reduce | bytes 65538
  35.6 2.6 %reshape.63 = bf16[16,2,512]{2,1,0:T(2,128)(2,1)} reshape(bf16[4096,4]{1,0:T(8,128)(2,1)S(1)} %reduce) | data formatting | bytes 65536
  38.1 7.4 %all-to-all-start = ((bf16[16,2,512]{2,1,0:T(2,128)(2,1)}), bf16[16,2,512]{2,1,0:T(2,128)(2,1)S(1)}, u32[]{:S(2)}, u32[]{:S(2)}) async-start(bf16[16,2,512]{2,1,0:T(2,128)(2,1)} %reshape.63), calls=%async_computation | async-start | bytes 65536 | tf_op jit(solution)/shard_map/all_to_all | solution.py:44
  45.5 0.1 iota_compare_fusion
  45.6 0.5 convert_divide_fusion.1
  46.1 0.6 constant_dynamic-update-slice_fusion.15
  46.7 0.6 constant_dynamic-update-slice_fusion.14
  47.3 0.6 constant_dynamic-update-slice_fusion.13
  47.9 0.6 constant_dynamic-update-slice_fusion.12
  48.5 0.6 constant_dynamic-update-slice_fusion.11
  49.1 0.6 constant_dynamic-update-slice_fusion.10
  49.7 0.6 constant_dynamic-update-slice_fusion.9
  50.3 0.6 constant_dynamic-update-slice_fusion.8
  50.9 0.6 constant_dynamic-update-slice_fusion.7
  51.5 0.6 constant_dynamic-update-slice_fusion.6
  52.1 0.6 constant_dynamic-update-slice_fusion.5
  52.7 0.6 constant_dynamic-update-slice_fusion.4
  53.3 0.6 constant_dynamic-update-slice_fusion.3
  53.9 0.6 constant_dynamic-update-slice_fusion.2
  54.5 0.6 constant_dynamic-update-slice_fusion.1
  55.1 0.6 constant_dynamic-update-slice_fusion
  55.7 0.6 lt.31
  56.3 1.5 fusion
  57.9 0.5 iota_add_fusion
  58.4 6.0 %all-to-all-start.1 = ((bf16[16,4,1,896]{3,1,2,0:T(4,128)(2,1)}), bf16[16,4,1,896]{3,1,2,0:T(4,128)(2,1)S(1)}, u32[]{:S(2)}, u32[]{:S(2)}) async-start(bf16[16,4,1,896]{3,1,2,0:T(4,128)(2,1)} %constant_dynamic-update-slice_fusion), calls=%async_computation.1 | async-start | bytes 229376 | tf_op jit(solution)/shard_map/all_to_all | solution.py:39
  64.4 0.0 copy-start.1
  64.4 0.0 reduce-scatter.4.cloned.1.call-start
  64.5 4.5 %reshape.64 = bf16[4096,1,4]{2,1,0:T(2,128)(2,1)} reshape(bf16[16,2,512]{2,1,0:T(2,128)(2,1)S(1)} %all-to-all-done) | data formatting | bytes 65536
  69.0 4.5 %copy.35 = bf16[4,1,4096]{2,0,1:T(4,128)(2,1)S(1)} copy(bf16[4,1,4096]{0,1,2:T(2,128)(2,1)} %bitcast.103) | data formatting | bytes 65536 | tf_op jit(solution)/shard_map/all_to_all | solution.py:44
  73.5 0.6 reshape.43
  74.2 1.9 %convolution_bitcast_fusion = f32[1024,64]{1,0:T(8,128)} fusion(bf16[64,256]{1,0:T(8,128)(2,1)} %reshape.43, bf16[1,256,1024]{2,1,0:T(8,128)(2,1)S(1)} %copy-done.1), kind=kOutput, calls=%fused_computation.5 | convolution fusion | flops 33554432 | bytes 819200
  76.1 0.0 reduce-scatter.4.cloned.1.call-update
  76.1 0.0 all-to-all-done.1
  76.2 0.5 fusion.1
  76.6 0.0 copy-start.6
  76.6 0.0 copy-start.8
  76.7 64.7 %all-reduce.1 = bf16[64,1024]{1,0:T(8,128)(2,1)S(1)} all-reduce(f32[64,1024]{1,0:T(8,128)S(1)} %fusion.1), channel_id=1, replica_groups=mesh['section'=2,'dp'=16] {'dp'}, use_global_device_ids=true, to_apply=%region_1.0 | all-reduce | flops 65536 | bytes 393216 | tf_op jit(solution)/shard_map/psum | solution.py:61
  141.4 0.0 reduce-scatter.4.cloned.1.call-done
  141.4 0.8 copy.40
  142.2 0.1 convert_select_fusion
  142.3 0.0 copy-done.4
  142.3 0.3 convolution_multiply_fusion
  142.7 3.5 %convolution_bitcast_fusion.1 = f32[4,8]{1,0:T(4,128)S(1)} fusion(bf16[8,64,1024]{2,1,0:T(8,128)(2,1)S(1)} %fusion, f32[4,64,1024]{2,1,0:T(8,128)S(1)} %convolution_multiply_fusion), kind=kOutput, calls=%fused_computation.8 | convolution fusion | flops 25165824 | bytes 2097280 | tf_op jit(solution)/shard_map/mij,qij->mq/dot_general | solution.py:79
  146.2 29.5 %psum.15 = f32[4,8]{1,0:T(4,128)S(1)} all-reduce(f32[4,8]{1,0:T(4,128)S(1)} %convolution_bitcast_fusion.1), channel_id=1, replica_groups=mesh['section'=2,'dp'=16] {'dp'}, use_global_device_ids=true, to_apply=%region_2.3 | all-reduce | flops 32 | bytes 256 | tf_op jit(solution)/shard_map/psum | solution.py:84
  175.7 4.4 %all-gather.1 = f32[2,4,8]{2,1,0:T(4,128)S(1)} all-gather(f32[1,4,8]{2,1,0:T(4,128)S(1)} %bitcast.126), channel_id=2, replica_groups=mesh['section'=2,'dp'=16] {'section'}, dimensions={0}, use_global_device_ids=true | all-gather | bytes 384 | tf_op jit(solution)/shard_map/all_gather | solution.py:11
  180.0 0.8 fusion.3
  (19 shorter events, 0.1 us)
Async XLA Ops:
  6.5 69.6 %copy-start = (bf16[1,896,1024]{2,1,0:T(8,128)(2,1)S(1)}, bf16[1,896,1024]{2,1,0:T(8,128)(2,1)}, u32[]{:S(2)}) copy-start(bf16[1,896,1024]{2,1,0:T(8,128)(2,1)} %param.11) | copy-start | bytes 5505028
  12.0 33.5 %copy-start.7 = (s32[4]{0:T(128)S(1)}, s32[4]{0:T(128)}, u32[]{:S(2)}) copy-start(s32[4]{0:T(128)} %param.15) | copy-start | bytes 52
  12.1 34.1 %copy-start.3 = (bf16[1,4,1,14336]{3,1,2,0:T(4,128)(2,1)S(1)}, bf16[1,4,1,14336]{3,1,2,0:T(4,128)(2,1)}, u32[]{:S(2)}) copy-start(bf16[1,4,1,14336]{3,1,2,0:T(4,128)(2,1)} %param.9) | copy-start | bytes 344068
  12.1 44.2 %copy-start.2 = (f32[1,64,1024]{2,1,0:T(8,128)S(1)}, f32[1,64,1024]{2,1,0:T(8,128)}, u32[]{:S(2)}) copy-start(f32[1,64,1024]{2,1,0:T(8,128)} %param.13) | copy-start | bytes 786436
  38.1 20.3 %all-to-all-start = ((bf16[16,2,512]{2,1,0:T(2,128)(2,1)}), bf16[16,2,512]{2,1,0:T(2,128)(2,1)S(1)}, u32[]{:S(2)}, u32[]{:S(2)}) async-start(bf16[16,2,512]{2,1,0:T(2,128)(2,1)} %reshape.63), calls=%async_computation | async-start | bytes 65536 | tf_op jit(solution)/shard_map/all_to_all | solution.py:44
  58.4 17.7 %all-to-all-start.1 = ((bf16[16,4,1,896]{3,1,2,0:T(4,128)(2,1)}), bf16[16,4,1,896]{3,1,2,0:T(4,128)(2,1)S(1)}, u32[]{:S(2)}, u32[]{:S(2)}) async-start(bf16[16,4,1,896]{3,1,2,0:T(4,128)(2,1)} %constant_dynamic-update-slice_fusion), calls=%async_computation.1 | async-start | bytes 229376 | tf_op jit(solution)/shard_map/all_to_all | solution.py:39
  64.4 9.8 %copy-start.1 = (bf16[1,256,1024]{2,1,0:T(8,128)(2,1)S(1)}, bf16[1,256,1024]{2,1,0:T(8,128)(2,1)}, u32[]{:S(2)}) copy-start(bf16[1,256,1024]{2,1,0:T(8,128)(2,1)} %param.12) | copy-start | bytes 1572868
  64.4 76.9 %reduce-scatter.4.cloned.1.call-start = ((), (), s32[]{:S(2)}) async-start(), calls=%async_computation.3 | async-start | bytes 557056
  74.2 68.0 %copy-start.5 = (pred[64]{0:T(512)(128)(4,1)S(1)}, pred[64]{0:T(512)(128)(4,1)}, u32[]{:S(2)}) copy-start(pred[64]{0:T(512)(128)(4,1)} %lt.31) | copy-start | bytes 196
  74.2 68.1 %copy-start.4 = (f32[4]{0:T(128)S(1)}, f32[4]{0:T(128)}, u32[]{:S(2)}) copy-start(f32[4]{0:T(128)} %convert_divide_fusion.1) | copy-start | bytes 52
  76.6 103.4 %copy-start.6 = (f32[8,8]{1,0:T(8,128)S(1)}, f32[8,8]{1,0:T(8,128)}, u32[]{:S(2)}) copy-start(f32[8,8]{1,0:T(8,128)} %param.17) | copy-start | bytes 772
  76.6 103.4 %copy-start.8 = (s32[4]{0:T(128)S(1)}, s32[4]{0:T(128)}, u32[]{:S(2)}) copy-start(s32[4]{0:T(128)} %param.16) | copy-start | bytes 52
  76.6 103.4 %copy-start.9 = (s32[8]{0:T(128)S(1)}, s32[8]{0:T(128)}, u32[]{:S(2)}) copy-start(s32[8]{0:T(128)} %iota_add_fusion) | copy-start | bytes 100
Sparse Core Ops, SparseCore 0:
  76.2 57.6 reduce-scatter.3
